TPU v7x, 32 devices: a whole 2x2x4 slice. The times are simulated.
32 devices in a mesh: dp: 16 (over z, x, core), tp: 2 (over y).
Axes of the slice: x: 2, y: 2, z: 4, core: 2. Of those that a mesh axis runs over, the one named last changes fastest.
Arguments:
- hidden: bfloat16 [512, 4096], P('dp', 'tp'), may hold values from -6 to 6
- routes: int32 [512, 8], P('dp'), may hold values from 0 to 15, all different within a row; in each aligned block of 32 rows (0 to 31, 32 to 63, ...) at most 32 rows name the same one
- routing_weights: float32 [512, 8], P('dp'), may hold values from 0.05 to 1
- w_gate: bfloat16 [16, 4096, 1536], P('dp', None, 'tp'), may hold values from -0.09375 to 0.09375
- w_up: bfloat16 [16, 4096, 1536], P('dp', None, 'tp'), may hold values from -0.09375 to 0.09375
- w_down: bfloat16 [16, 1536, 4096], P('dp', 'tp'), may hold values from -0.15625 to 0.15625
- norm_gain: float32 [4096], replicated, may hold values from 0.1 to 1.9
- key_projection_weight: bfloat16 [4096, 512], P(None, 'tp'), may hold values from -0.09375 to 0.09375
- value_projection_weight: bfloat16 [4096, 512], P(None, 'tp'), may hold values from -0.09375 to 0.09375
- queries: bfloat16 [512, 8192], P('dp', 'tp'), may hold values from -128 to 128
- cached_key_rows: bfloat16 [16, 128, 512], P('dp', None, 'tp'), may hold values from -4 to 4
- cached_value_rows: bfloat16 [16, 128, 512], P('dp', None, 'tp'), may hold values from -6 to 6
- lengths: int32 [16], P('dp'), may hold values from 16 to 128
- parents: int32 [16, 32], P('dp'), may hold values from -1 to 30, as said below
Outputs:
- layer_output: bfloat16 [512, 4096], P('dp', 'tp')
- next_layer_keys: bfloat16 [512, 512], P('dp', 'tp')
- next_layer_values: bfloat16 [512, 512], P('dp', 'tp')
- attended: bfloat16 [512, 8192], P('dp', 'tp')
Inputs may be any that keep to these rules, and one draw needn't show every extreme that they name: `routes`: each row names 8 different experts. In each aligned block of 32 rows (the rows of one device) no expert is named by more than 32 rows, a bound that some block reaches. `parents`: node 0 of each request is the root, with parent -1; every other node i has its parent among nodes max(0, i - 8) to i - 1.
All inputs are finite; a program needn't handle non-finite values.
Results may differ from a plain program's by a relative error of at most 0.013.
Values may be sent and summed in bfloat16 or wider, within the bound.
A program may use at most 64 MiB of HBM per device.

v0:
```python
import math

import jax
import jax.numpy as jnp
from jax import lax
from jax.sharding import PartitionSpec as P

HEAD_SIZE = 128


def ancestry(parent_row):
    node_count = parent_row.shape[0]
    position = jnp.arange(node_count, dtype=jnp.int32)
    reached = (parent_row[:, None] == position[None, :]).astype(jnp.float32)
    reached = reached + jnp.eye(node_count, dtype=jnp.float32)
    for doubling in range((node_count - 1).bit_length()):
        reached = jnp.minimum(jnp.dot(reached, reached, preferred_element_type=jnp.float32), 1.0)
    return reached > 0.5


def full_rows(hidden):
    return lax.all_gather(hidden, "tp", axis=1, tiled=True)


def attend_local(
    queries, cached_key_rows, cached_value_rows, tree_key_rows, tree_value_rows, lengths, parents
):
    request_count = lengths.shape[0]
    node_count = parents.shape[1]
    slot_length = cached_key_rows.shape[1]
    kv_local = cached_key_rows.shape[2] // HEAD_SIZE
    query_group_count = queries.shape[1] // (kv_local * HEAD_SIZE)
    scaled = 1.0 / math.sqrt(HEAD_SIZE)
    tree_query_block = queries.reshape(
        request_count, node_count, kv_local, query_group_count, HEAD_SIZE
    )
    joined_key_block = cached_key_rows.reshape(request_count, slot_length, kv_local, HEAD_SIZE)
    joined_value_block = cached_value_rows.reshape(request_count, slot_length, kv_local, HEAD_SIZE)
    tree_key_block = tree_key_rows.reshape(request_count, node_count, kv_local, HEAD_SIZE)
    tree_value_block = tree_value_rows.reshape(request_count, node_count, kv_local, HEAD_SIZE)
    cache_scores = (
        jnp.einsum(
            "rnkgd,rpkd->rkgnp",
            tree_query_block,
            joined_key_block,
            preferred_element_type=jnp.float32,
        )
        * scaled
    )
    tree_scores = (
        jnp.einsum(
            "rnkgd,rmkd->rkgnm",
            tree_query_block,
            tree_key_block,
            preferred_element_type=jnp.float32,
        )
        * scaled
    )
    visible = jnp.arange(slot_length, dtype=jnp.int32)[None, :] < lengths[:, None]
    cache_scores = jnp.where(visible[:, None, None, None, :], cache_scores, -1e30)
    related = jax.vmap(ancestry)(parents)
    tree_scores = jnp.where(related[:, None, None], tree_scores, -1e30)
    highest = jnp.maximum(jnp.max(cache_scores, axis=-1), jnp.max(tree_scores, axis=-1))[..., None]
    cache_raised = jnp.exp(cache_scores - highest)
    tree_raised = jnp.exp(tree_scores - highest)
    denominator = jnp.sum(cache_raised, axis=-1, keepdims=True) + jnp.sum(
        tree_raised, axis=-1, keepdims=True
    )
    cache_weights = (cache_raised / denominator).astype(jnp.bfloat16)
    tree_weights = (tree_raised / denominator).astype(jnp.bfloat16)
    output = jnp.einsum(
        "rkgnp,rpkd->rnkgd", cache_weights, joined_value_block, preferred_element_type=jnp.float32
    )
    output = output + jnp.einsum(
        "rkgnm,rmkd->rnkgd", tree_weights, tree_value_block, preferred_element_type=jnp.float32
    )
    return output.reshape(request_count * node_count, -1).astype(jnp.bfloat16)


def on_device(
    hidden,
    routes,
    routing_weights,
    w_gate,
    w_up,
    w_down,
    norm_gain,
    key_projection_weight,
    value_projection_weight,
    queries,
    cached_key_rows,
    cached_value_rows,
    lengths,
    parents,
):
    token_count = hidden.shape[0]
    top_count = routes.shape[1]
    local_experts = w_gate.shape[0]
    expert_count = lax.axis_size("dp") * local_experts
    capacity = min(token_count, 2 * token_count * top_count // expert_count)
    weights = routing_weights / jnp.sum(routing_weights, axis=1, keepdims=True)
    flat_routes = routes.reshape(-1)
    expert_ids = jnp.arange(expert_count, dtype=jnp.int32)
    matches = (flat_routes[:, None] == expert_ids[None, :]).astype(jnp.int32)
    running = jnp.cumsum(matches, axis=0)
    slot_index = jnp.sum(matches * running, axis=1) - 1
    targets = flat_routes * capacity + slot_index
    owners = jnp.arange(token_count * top_count, dtype=jnp.int32) // top_count
    token_table = (
        jnp.full((expert_count * capacity,), token_count, jnp.int32).at[targets].set(owners)
    )
    whole_rows = None
    whole_rows = full_rows(hidden)
    padded = jnp.concatenate(
        [whole_rows, jnp.zeros((1, whole_rows.shape[1]), whole_rows.dtype)], axis=0
    )
    outgoing = jnp.take(padded, token_table, axis=0).reshape(
        expert_count, capacity, whole_rows.shape[1]
    )
    received = lax.all_to_all(outgoing, "dp", split_axis=0, concat_axis=0, tiled=True)
    slot_count = received.shape[1]
    grouped = received.reshape(-1, local_experts, slot_count, received.shape[2])
    gate_act = jnp.einsum("secd,edf->secf", grouped, w_gate, preferred_element_type=jnp.float32)
    upward = jnp.einsum("secd,edf->secf", grouped, w_up, preferred_element_type=jnp.float32)
    active = (jax.nn.silu(gate_act) * upward).astype(jnp.bfloat16)
    partial_value = jnp.einsum("secf,efd->secd", active, w_down, preferred_element_type=jnp.float32)
    partial_value = partial_value.reshape(received.shape[0], slot_count, partial_value.shape[3])
    summed = lax.psum_scatter(
        partial_value.astype(jnp.bfloat16), "tp", scatter_dimension=2, tiled=True
    ).astype(jnp.float32)
    back = lax.all_to_all(
        summed.astype(jnp.bfloat16), "dp", split_axis=0, concat_axis=0, tiled=True
    ).astype(summed.dtype)
    flat_back = back.reshape(expert_count * capacity, back.shape[2])
    picked = jnp.take(flat_back, targets, axis=0).reshape(token_count, top_count, back.shape[2])
    expert_mix = jnp.sum(weights[:, :, None] * picked, axis=1)
    own_out = (hidden.astype(jnp.float32) + expert_mix).astype(jnp.bfloat16)
    full_out = lax.all_gather(own_out, "tp", axis=1, tiled=True)
    widened = full_out.astype(jnp.float32)
    scaling = lax.rsqrt(jnp.mean(widened * widened, axis=1, keepdims=True) + 1e-06)
    normed = (widened * scaling * norm_gain).astype(jnp.bfloat16)
    tree_key_rows = jnp.dot(
        normed, key_projection_weight, preferred_element_type=jnp.float32
    ).astype(jnp.bfloat16)
    tree_value_rows = jnp.dot(
        normed, value_projection_weight, preferred_element_type=jnp.float32
    ).astype(jnp.bfloat16)
    attended = attend_local(
        queries,
        cached_key_rows,
        cached_value_rows,
        tree_key_rows,
        tree_value_rows,
        lengths,
        parents,
    )
    return (own_out, tree_key_rows, tree_value_rows, attended)


def solution(mesh):
    return jax.shard_map(
        on_device,
        mesh=mesh,
        in_specs=(
            P("dp", "tp"),
            P("dp", None),
            P("dp", None),
            P("dp", None, "tp"),
            P("dp", None, "tp"),
            P("dp", "tp", None),
            P(),
            P(None, "tp"),
            P(None, "tp"),
            P("dp", "tp"),
            P("dp", None, "tp"),
            P("dp", None, "tp"),
            P("dp"),
            P("dp", None),
        ),
        out_specs=(P("dp", "tp"), P("dp", "tp"), P("dp", "tp"), P("dp", "tp")),
        check_vma=False,
    )
```

profile of v0, /device:TPU:0, one launch (start us, length us, event | category | flops | bytes accessed | tf_op | source)
XLA Modules:
  0.0 285.8 jit_solution(1496467030900741611)
XLA Ops:
  7.2 0.9 copy.29
  8.3 0.6 reduce-window.6
  8.9 0.2 slice_reduce_fusion
  9.4 1.4 scatter_custom_fusion
  10.8 7.4 %all_gather.6 = bf16[32,4096]{1,0:T(8,128)(2,1)S(1)} all-gather(bf16[32,2048]{1,0:T(8,128)(2,1)} %param.14), channel_id=1, replica_groups=mesh['dp'=16,'tp'=2] {'tp'}, dimensions={1}, use_global_device_ids=true | all-gather | bytes 393216 | tf_op jit(solution)/shard_map/all_gather | solution.py:22
  18.3 4.4 %gather_fusion = bf16[512,4096]{1,0:T(8,128)(2,1)} fusion(bf16[33,4096]{1,0:T(8,128)(2,1)S(1)} %concatenate.3, s32[1024]{0:T(1024)S(1)} %pad_clamp_fusion.1), kind=kCustom, calls=%fused_computation | custom fusion | bytes 8390656 | tf_op jit(solution)/shard_map/jit(_take)/gather | solution.py:117
  22.7 2.6 broadcast_select_fusion
  25.3 98.0 %all_to_all.10 = bf16[16,32,4096]{2,1,0:T(8,128)(2,1)S(1)} all-to-all(bf16[16,32,4096]{2,1,0:T(8,128)(2,1)S(1)} %broadcast_select_fusion), channel_id=1, replica_groups=mesh['dp'=16,'tp'=2] {'dp'}, dimensions={0} | all-to-all | bytes 8388608 | tf_op jit(solution)/shard_map/all_to_all | solution.py:120
  123.3 2.0 copy-done.1
  125.3 6.8 %fusion.4 = f32[16,32,768]{2,1,0:T(8,128)} fusion(bf16[16,32,4096]{2,1,0:T(8,128)(2,1)S(1)} %all_to_all.10, bf16[1,4096,768]{2,1,0:T(8,128)(2,1)} %param.17), kind=kOutput, calls=%fused_computation.7 | convolution fusion | flops 3221225472 | bytes 12058624 | tf_op jit(solution)/shard_map/secd,edf->secf/dot_general | solution.py:123
  132.0 17.0 %fusion.6 = bf16[16,32,4096]{2,1,0:T(8,128)(2,1)} fusion(bf16[1,768,4096]{2,1,0:T(8,128)(2,1)} %param.19, bf16[16,32,4096]{2,1,0:T(8,128)(2,1)} %copy-done.1, bf16[1,4096,768]{2,1,0:T(8,128)(2,1)} %param.18, f32[16,32,768]{2,1,0:T(8,128)} %fusion.4), kind=kOutput, calls=%fused_computation.9 | convolution fusion | flops 6446907392 | bytes 22544384 | tf_op jit(solution)/shard_map/secf,efd->secd/dot_general | solution.py:126
  149.1 55.2 %reduce-scatter.2.cloned.1.call-done = bf16[16,32,2048]{2,1,0:T(8,128)(2,1)} async-done(((bf16[16,32,4096]{2,1,0:T(8,128)(2,1)}), bf16[16,32,2048]{2,1,0:T(8,128)(2,1)}) %reduce-scatter.2.cloned.1.call-update) | async-done | bytes 2097168 | tf_op jit(solution)/shard_map/reduce_scatter | solution.py:128
  204.3 5.7 %all-to-all-start.1 = ((bf16[16,32,2048]{2,1,0:T(8,128)(2,1)}), bf16[16,32,2048]{2,1,0:T(8,128)(2,1)}, u32[]{:S(2)}, u32[]{:S(2)}) async-start(bf16[16,32,2048]{2,1,0:T(8,128)(2,1)} %reduce-scatter.2.cloned.1.call-done), calls=%async_computation.2 | async-start | bytes 4194304 | tf_op jit(solution)/shard_map/all_to_all | solution.py:131
  210.4 0.1 convolution_minimum_fusion.4
  210.5 0.2 convolution_minimum_fusion.2
  210.8 0.2 fusion.29
  211.9 1.1 fusion.59
  213.0 38.1 %all-to-all-done.1 = bf16[16,32,2048]{2,1,0:T(8,128)(2,1)} async-done(((bf16[16,32,2048]{2,1,0:T(8,128)(2,1)}), bf16[16,32,2048]{2,1,0:T(8,128)(2,1)}, u32[]{:S(2)}, u32[]{:S(2)}) %all-to-all-start.1) | async-done | bytes 2097184 | tf_op jit(solution)/shard_map/all_to_all | solution.py:131
  251.0 4.0 %bitcast_convert_fusion = f32[512,2048]{1,0:T(8,128)} fusion(bf16[16,32,2048]{2,1,0:T(8,128)(2,1)} %all-to-all-done.1), kind=kLoop, calls=%fused_computation.11 | loop fusion | flops 1048576 | bytes 6291456 | tf_op jit(solution)/shard_map/reshape | solution.py:134
  255.1 5.8 %gather_fusion.1 = f32[256,2048]{1,0:T(8,128)} fusion(f32[512,2048]{1,0:T(8,128)} %bitcast_convert_fusion, s32[1024]{0:T(1024)S(1)} %pad_clamp_fusion), kind=kCustom, calls=%fused_computation.1 | custom fusion | bytes 4195328 | tf_op jit(solution)/shard_map/jit(_take)/gather | solution.py:135
  260.9 3.2 %fusion.10 = f32[32,2048]{1,0:T(8,128)S(1)} fusion(f32[256,2048]{1,0:T(8,128)} %gather_fusion.1, f32[32,8]{1,0:T(8,128)S(1)} %copy.28, pred[32,8]{1,0:T(8,128)(4,1)S(1)} %compare_and_fusion), kind=kLoop, calls=%fused_computation.14 | loop fusion | flops 1507328 | bytes 2360576 | tf_op jit(solution)/shard_map/reduce_sum | solution.py:136
  264.2 7.0 %all_gather.7 = bf16[32,4096]{1,0:T(8,128)(2,1)S(1)} all-gather(bf16[32,2048]{1,0:T(8,128)(2,1)S(1)} %add_convert_fusion), channel_id=1, replica_groups=mesh['dp'=16,'tp'=2] {'tp'}, dimensions={1}, use_global_device_ids=true | all-gather | bytes 393216 | tf_op jit(solution)/shard_map/all_gather | solution.py:138
  271.2 0.2 fusion.31
  271.4 0.5 convolution_convert_fusion.1
  271.9 0.5 fusion.60
  272.5 0.1 fusion.35
  272.6 1.4 fusion.34
  274.1 2.1 convolution_convert_fusion
  276.2 1.5 convolution_bitcast_fusion
  277.7 0.3 fusion.28
  278.0 0.1 copy.41
  278.1 0.8 convert_element_type.113
  (59 shorter events, 1.2 us)
Async XLA Ops:
  7.2 264.2 %copy-start = (bf16[4096,256]{1,0:T(8,128)(2,1)S(1)}, bf16[4096,256]{1,0:T(8,128)(2,1)}, u32[]{:S(2)}) copy-start(bf16[4096,256]{1,0:T(8,128)(2,1)} %param.21) | copy-start | bytes 6291460
  7.2 197.1 %reduce-scatter.2.cloned.1.call-start = ((), (), s32[]{:S(2)}) async-start(), calls=%async_computation.3 | async-start | bytes 6291456 | tf_op jit(solution)/shard_map/reduce_scatter | solution.py:128
  123.3 2.0 copy-start.1
  149.0 61.1 %copy-start.10 = (f32[32,8]{0,1:T(8,128)S(1)}, f32[32,8]{0,1:T(8,128)}, u32[]{:S(2)}) copy-start(f32[32,8]{0,1:T(8,128)} %param.16) | copy-start | bytes 3076
  149.0 61.2 %copy-start.4 = (bf16[32,4096]{1,0:T(8,128)(2,1)S(1)}, bf16[32,4096]{1,0:T(8,128)(2,1)}, u32[]{:S(2)}) copy-start(bf16[32,4096]{1,0:T(8,128)(2,1)} %param.23) | copy-start | bytes 786436
  149.0 61.3 %copy-start.11 = (s32[1,32]{1,0:T(1,128)S(1)}, s32[1,32]{1,0:T(1,128)}, u32[]{:S(2)}) copy-start(s32[1,32]{1,0:T(1,128)} %param.27) | copy-start | bytes 388
  149.0 62.1 %copy-start.8 = (bf16[1,128,256]{2,1,0:T(8,128)(2,1)S(1)}, bf16[1,128,256]{2,1,0:T(8,128)(2,1)}, u32[]{:S(2)}) copy-start(bf16[1,128,256]{2,1,0:T(8,128)(2,1)} %param.24) | copy-start | bytes 196612
  149.0 62.8 %copy-start.9 = (bf16[1,128,256]{2,1,0:T(8,128)(2,1)S(1)}, bf16[1,128,256]{2,1,0:T(8,128)(2,1)}, u32[]{:S(2)}) copy-start(bf16[1,128,256]{2,1,0:T(8,128)(2,1)} %param.25) | copy-start | bytes 196612
  204.3 46.7 %all-to-all-start.1 = ((bf16[16,32,2048]{2,1,0:T(8,128)(2,1)}), bf16[16,32,2048]{2,1,0:T(8,128)(2,1)}, u32[]{:S(2)}, u32[]{:S(2)}) async-start(bf16[16,32,2048]{2,1,0:T(8,128)(2,1)} %reduce-scatter.2.cloned.1.call-done), calls=%async_computation.2 | async-start | bytes 4194304 | tf_op jit(solution)/shard_map/all_to_all | solution.py:131
  255.1 9.0 %copy-start.2 = (bf16[32,2048]{1,0:T(8,128)(2,1)S(1)}, bf16[32,2048]{1,0:T(8,128)(2,1)}, u32[]{:S(2)}) copy-start(bf16[32,2048]{1,0:T(8,128)(2,1)} %param.14) | copy-start | bytes 393220
  255.1 16.3 %copy-start.5 = (f32[4096]{0:T(1024)S(1)}, f32[4096]{0:T(1024)}, u32[]{:S(2)}) copy-start(f32[4096]{0:T(1024)} %param.20) | copy-start | bytes 49156
  264.2 13.5 %copy-start.3 = (bf16[32,2048]{1,0:T(8,128)(2,1)}, bf16[32,2048]{1,0:T(8,128)(2,1)S(1)}, u32[]{:S(2)}) copy-start(bf16[32,2048]{1,0:T(8,128)(2,1)S(1)} %add_convert_fusion) | copy-start | bytes 393220
  271.9 6.1 %copy-start.6 = (bf16[32,256]{1,0:T(8,128)(2,1)}, bf16[32,256]{1,0:T(8,128)(2,1)S(1)}, u32[]{:S(2)}) copy-start(bf16[32,256]{1,0:T(8,128)(2,1)S(1)} %convolution_convert_fusion.1) | copy-start | bytes 49156
  276.1 2.8 copy-start.7
Sparse Core Ops, SparseCore 0:
  149.2 55.0 reduce-scatter.1
where the time goes:
time: 291 us; the launch traced here: 286 us
  blocking collectives  112 us (38%)
  waiting for transfers between devices  93.3 us (32%)
  matrix products  30.4 us (10%)
  local copies, waits for them, and re-layouts  16.4 us (6%)
  between operations  15 us (5%)
  other arithmetic  12.5 us (4%)
  starting transfers between devices  5.74 us (2%)
    all_to_all x1, blocking collectives, on_device(): lax.all_to_all(outgoing, 'dp', split_axis=0, concat_axis=0, tiled=True)  98 us
    reduce_scatter x1, waiting for transfers between devices, on_device(): lax.psum_scatter(partial_value.astype(jnp.bfloat16), 'tp', scatter_dimens...  55.2 us
    all_to_all x1, waiting for transfers between devices, on_device(): lax.all_to_all(summed.astype(jnp.bfloat16), 'dp', split_axis=0, concat_ax...  38.1 us
    dot_general x1, matrix products, on_device(): jnp.einsum('secf,efd->secd', active, w_down, preferred_element_type=jnp.f...  17 us
    all_gather x1, blocking collectives, full_rows(): return lax.all_gather(hidden, 'tp', axis=1, tiled=True)  7.42 us
    all_gather x1, blocking collectives, on_device(): full_out = lax.all_gather(own_out, 'tp', axis=1, tiled=True)  7.03 us
    dot_general x1, matrix products, on_device(): jnp.einsum('secd,edf->secf', grouped, w_gate, preferred_element_type=jnp....  6.77 us
    gather x1, local copies, waits for them, and re-layouts, on_device(): jnp.take(flat_back, targets, axis=0)  5.83 us
  transfers between devices with their start and end apart: 2, of which 2 were waited for; matrix products, arithmetic and copies ran while one was open for 1% of the time, Pallas kernels for 0%

commit v1 on v0

--- a/solution.py
+++ b/solution.py
@@ -1,8 +1,12 @@
 import math
+
+import functools
 
 import jax
 import jax.numpy as jnp
 from jax import lax
+from jax.experimental import pallas as pl
+from jax.experimental.pallas import tpu as pltpu
 from jax.sharding import PartitionSpec as P
 
 HEAD_SIZE = 128
@@ -16,6 +20,331 @@
     for doubling in range((node_count - 1).bit_length()):
         reached = jnp.minimum(jnp.dot(reached, reached, preferred_element_type=jnp.float32), 1.0)
     return reached > 0.5
+
+CORES = 2
+COLUMNS = 2
+PIECES = 8
+
+
+def expert_kernel(
+    planes,
+    hidden_ref,
+    share_ref,
+    gate_ref,
+    up_ref,
+    down_ref,
+    own_ref,
+    full_ref,
+    rows,
+    shares,
+    gate,
+    up,
+    down,
+    gate_total,
+    up_total,
+    active,
+    factor,
+    mixed,
+    from_core,
+    from_first,
+    from_second,
+    from_plane,
+    whole,
+    local_sems,
+    send_sems,
+    recv_sems,
+):
+    me = lax.axis_index("dp")
+    side = lax.axis_index("tp")
+    core = lax.rem(me, CORES)
+    column = lax.rem(me // CORES, COLUMNS)
+    plane = me // (CORES * COLUMNS)
+    pieces = rows.shape[0]
+    width = rows.shape[-1]
+    row_count = rows.shape[2] * rows.shape[3] * rows.shape[4] * rows.shape[5]
+    half = pieces * width
+    ff = gate.shape[-1]
+
+    def device(plane_, column_, core_, side_):
+        return ((plane_ * COLUMNS + column_) * CORES + core_, side_)
+
+    over_core = device(plane, column, 1 - core, side)
+    over_column = device(plane, 1 - column, core, side)
+    over_side = device(plane, column, core, 1 - side)
+    others = [lax.rem(plane + k, planes) for k in range(1, planes)]
+    over_planes = [device(o, column, core, side) for o in others]
+
+    local_count = [0]
+
+    def local(source, target):
+        copy = pltpu.make_async_copy(source, target, local_sems.at[local_count[0]])
+        local_count[0] += 1
+        copy.start()
+        return copy
+
+    own_loads = [
+        local(
+            hidden_ref.at[:, pl.ds(p * width, width)], rows.at[p, side, core, column, plane]
+        )
+        for p in range(pieces)
+    ]
+    share_load = local(share_ref, shares.at[core, column, plane])
+
+    barrier = pltpu.get_barrier_semaphore()
+    partners = over_planes + [over_column, over_side, over_core]
+    for partner in partners:
+        pl.semaphore_signal(
+            barrier, inc=1, device_id=partner, device_id_type=pl.DeviceIdType.MESH
+        )
+    for copy in own_loads:
+        copy.wait()
+    share_load.wait()
+    pl.semaphore_wait(barrier, len(partners))
+
+    remote_count = [0]
+    sent = []
+
+    def remote(source, target, where):
+        index = remote_count[0]
+        remote_count[0] += 1
+        copy = pltpu.make_async_remote_copy(
+            src_ref=source,
+            dst_ref=target,
+            send_sem=send_sems.at[index],
+            recv_sem=recv_sems.at[index],
+            device_id=where,
+            device_id_type=pl.DeviceIdType.MESH,
+        )
+        copy.start()
+        sent.append(copy)
+        return copy
+
+    share_slot = shares.at[core, column, plane]
+    by_plane = {}
+    for p in range(pieces):
+        slot = rows.at[p, side, core, column, plane]
+        by_plane[p] = [remote(slot, slot, where) for where in over_planes]
+        if p == 0:
+            share_moves = [remote(share_slot, share_slot, where) for where in over_planes]
+
+    gate_loads, up_loads = [], []
+    for p in range(pieces):
+        gate_loads.append(local(gate_ref.at[:, p], gate.at[:, p]))
+        up_loads.append(local(up_ref.at[:, p], up.at[:, p]))
+    down_load = local(down_ref, down)
+
+    first, second, across = {}, {}, {}
+    tile = 256 if ff % 256 == 0 else ff
+
+    def multiply(p):
+        gate_loads[p].wait()
+        up_loads[p].wait()
+
+        def one(n, carry):
+            columns = pl.ds(pl.multiple_of(n * tile, tile), tile)
+            for weight, total in ((gate, gate_total), (up, up_total)):
+                added = None
+                for s in range(2):
+                    term = jnp.dot(
+                        rows[p, s].reshape(row_count, width),
+                        weight[s, p, :, columns],
+                        preferred_element_type=jnp.float32,
+                    )
+                    added = term if added is None else added + term
+                if p > 0:
+                    added = added + total[:, columns]
+                total[:, columns] = added
+            return carry
+
+        lax.fori_loop(0, ff // tile, one, 0)
+
+    for step in range(pieces + 3):
+        p = step
+        if p < pieces:
+            for copy in by_plane[p]:
+                copy.wait_recv()
+            block = rows.at[p, side, core, column]
+            first[p] = remote(block, block, over_column if p % 2 == 0 else over_side)
+            if p == 0:
+                for copy in share_moves:
+                    copy.wait_recv()
+                share_block = shares.at[core, column]
+                share_first = remote(share_block, share_block, over_column)
+        p = step - 1
+        if 0 <= p < pieces:
+            first[p].wait_recv()
+            if p % 2 == 0:
+                block = rows.at[p, side, core]
+                second[p] = remote(block, block, over_side)
+            else:
+                block = rows.at[p, :, core, column]
+                second[p] = remote(block, block, over_column)
+            if p == 0:
+                share_first.wait_recv()
+                share_across = remote(shares.at[core], shares.at[core], over_core)
+        p = step - 2
+        if 0 <= p < pieces:
+            second[p].wait_recv()
+            block = rows.at[p, :, core]
+            across[p] = remote(block, block, over_core)
+        p = step - 3
+        if 0 <= p < pieces:
+            across[p].wait_recv()
+            if p == 0:
+                share_across.wait_recv()
+                tokens, lanes = rows.shape[5], factor.shape[1]
+                diagonal = lax.broadcasted_iota(
+                    jnp.int32, (tokens, lanes), 0
+                ) == lax.broadcasted_iota(jnp.int32, (tokens, lanes), 1)
+                place = 0
+                for c in range(CORES):
+                    for x in range(COLUMNS):
+                        for z in range(planes):
+                            row = shares[c, x, z, pl.ds(me, 1), :]
+                            value = jnp.sum(
+                                jnp.where(diagonal, row, 0.0), axis=1, keepdims=True
+                            )
+                            factor[pl.ds(place * tokens, tokens), :] = jnp.broadcast_to(
+                                value, (tokens, lanes)
+                            )
+                            place += 1
+            multiply(p)
+
+    lanes = factor.shape[1]
+
+    def activate(n, carry):
+        columns = pl.ds(pl.multiple_of(n * lanes, lanes), lanes)
+        value = gate_total[:, columns]
+        value = value / (1.0 + jnp.exp(-value)) * up_total[:, columns] * factor[...]
+        active[:, columns] = value.astype(active.dtype)
+        return carry
+
+    lax.fori_loop(0, ff // lanes, activate, 0)
+    down_load.wait()
+
+    core_moves, first_moves, second_moves, plane_moves, side_moves = {}, {}, {}, {}, {}
+
+    def project(p):
+        def one(s, carry):
+            columns = pl.ds(pl.multiple_of(s * half + p * width, width), width)
+            value = jnp.dot(active[...], down[:, columns], preferred_element_type=jnp.float32)
+            mixed[p, s] = value.astype(mixed.dtype).reshape(mixed.shape[2:])
+            return carry
+
+        lax.fori_loop(0, 2, one, 0)
+        core_moves[p] = remote(mixed.at[p, :, 1 - core], from_core.at[p], over_core)
+
+    def add(target, other):
+        target[...] = (
+            target[...].astype(jnp.float32) + other[...].astype(jnp.float32)
+        ).astype(target.dtype)
+
+    for step in range(pieces + 5):
+        p = step
+        if p < pieces:
+            project(p)
+        p = step - 1
+        if 0 <= p < pieces:
+            core_moves[p].wait_recv()
+            add(mixed.at[p, :, core], from_core.at[p])
+            landing = from_first.at[p]
+            if p % 2 == 0:
+                first_moves[p] = remote(mixed.at[p, 1 - side, core], landing, over_side)
+            else:
+                first_moves[p] = remote(mixed.at[p, :, core, 1 - column], landing, over_column)
+        p = step - 2
+        if 0 <= p < pieces:
+            first_moves[p].wait_recv()
+            landing = from_second.at[p]
+            if p % 2 == 0:
+                add(mixed.at[p, side, core], from_first.at[p])
+                second_moves[p] = remote(
+                    mixed.at[p, side, core, 1 - column], landing, over_column
+                )
+            else:
+                add(mixed.at[p, :, core, column], from_first.at[p])
+                second_moves[p] = remote(
+                    mixed.at[p, 1 - side, core, column], landing, over_side
+                )
+        p = step - 3
+        if 0 <= p < pieces:
+            second_moves[p].wait_recv()
+            add(mixed.at[p, side, core, column], from_second.at[p])
+            plane_moves[p] = [
+                remote(mixed.at[p, side, core, column, o], from_plane.at[p, k], where)
+                for k, (o, where) in enumerate(zip(others, over_planes))
+            ]
+        p = step - 4
+        if 0 <= p < pieces:
+            total = mixed[p, side, core, column, plane].astype(jnp.float32)
+            for k, copy in enumerate(plane_moves[p]):
+                copy.wait_recv()
+                total = total + from_plane[p, k].astype(jnp.float32)
+            total = total + rows[p, side, core, column, plane].astype(jnp.float32)
+            total = total.astype(own_ref.dtype)
+            own_ref[:, pl.ds(p * width, width)] = total
+            whole[side, p] = total
+            side_moves[p] = remote(whole.at[side, p], whole.at[side, p], over_side)
+
+    for p in range(pieces):
+        side_moves[p].wait_recv()
+        for s in range(2):
+            full_ref[:, pl.ds(s * half + p * width, width)] = whole[s, p]
+    for copy in sent:
+        copy.wait_send()
+
+
+def dense_experts(hidden, shares, w_gate, w_up, w_down):
+    token_count, half = hidden.shape
+    expert_count = shares.shape[0]
+    planes = lax.axis_size("dp") // (CORES * COLUMNS)
+    ff = w_gate.shape[2]
+    pieces = PIECES
+    width = half // pieces
+    model_width = w_gate.shape[1]
+    gate = w_gate.reshape(2, pieces, width, ff)
+    up = w_up.reshape(2, pieces, width, ff)
+    down = w_down.reshape(ff, model_width)
+    lanes = shares.shape[1]
+    row_count = CORES * COLUMNS * planes * token_count
+    bf, f32 = jnp.bfloat16, jnp.float32
+    blocks = (token_count, width)
+    copies = pieces * (2 * (planes - 1) + 7) + planes + 1
+    anywhere = pl.BlockSpec(memory_space=pl.ANY)
+    inside = pl.BlockSpec(memory_space=pltpu.VMEM)
+    return pl.pallas_call(
+        functools.partial(expert_kernel, planes),
+        out_shape=(
+            jax.ShapeDtypeStruct((token_count, half), bf),
+            jax.ShapeDtypeStruct((token_count, 2 * half), bf),
+        ),
+        in_specs=[anywhere] * 5,
+        out_specs=(inside, inside),
+        scratch_shapes=[
+            pltpu.VMEM((pieces, 2, CORES, COLUMNS, planes, *blocks), bf),
+            pltpu.VMEM((CORES, COLUMNS, planes, expert_count, lanes), f32),
+            pltpu.VMEM((2, pieces, width, ff), bf),
+            pltpu.VMEM((2, pieces, width, ff), bf),
+            pltpu.VMEM((ff, model_width), bf),
+            pltpu.VMEM((row_count, ff), f32),
+            pltpu.VMEM((row_count, ff), f32),
+            pltpu.VMEM((row_count, ff), bf),
+            pltpu.VMEM((row_count, lanes), f32),
+            pltpu.VMEM((pieces, 2, CORES, COLUMNS, planes, *blocks), bf),
+            pltpu.VMEM((pieces, 2, COLUMNS, planes, *blocks), bf),
+            pltpu.VMEM((pieces, 2, planes, *blocks), bf),
+            pltpu.VMEM((pieces, planes, *blocks), bf),
+            pltpu.VMEM((pieces, planes - 1, *blocks), bf),
+            pltpu.VMEM((2, pieces, *blocks), bf),
+            pltpu.SemaphoreType.DMA((3 * pieces + 2,)),
+            pltpu.SemaphoreType.DMA((copies,)),
+            pltpu.SemaphoreType.DMA((copies,)),
+        ],
+        compiler_params=pltpu.CompilerParams(
+            collective_id=0, has_side_effects=True, vmem_limit_bytes=60 * 1024 * 1024
+        ),
+        name="dense_experts",
+    )(hidden, shares, gate, up, down)
 
 
 def full_rows(hidden):
@@ -77,28 +406,31 @@
     return output.reshape(request_count * node_count, -1).astype(jnp.bfloat16)
 
 
-def on_device(
-    hidden,
-    routes,
-    routing_weights,
-    w_gate,
-    w_up,
-    w_down,
-    norm_gain,
-    key_projection_weight,
-    value_projection_weight,
-    queries,
-    cached_key_rows,
-    cached_value_rows,
-    lengths,
-    parents,
-):
+LANES = 128
+
+
+def dense_fits(hidden, routes, w_gate):
+    token_count, half = hidden.shape
+    expert_count = lax.axis_size("dp") * w_gate.shape[0]
+    return (
+        2 * token_count * routes.shape[1] // expert_count >= token_count
+        and w_gate.shape[0] == 1
+        and lax.axis_size("tp") == 2
+        and lax.axis_size("dp") % (CORES * COLUMNS) == 0
+        and lax.axis_size("dp") > CORES * COLUMNS
+        and token_count % 16 == 0
+        and token_count <= LANES
+        and half % (PIECES * LANES) == 0
+        and w_gate.shape[2] % LANES == 0
+    )
+
+
+def routed_experts(hidden, routes, weights, w_gate, w_up, w_down):
     token_count = hidden.shape[0]
     top_count = routes.shape[1]
     local_experts = w_gate.shape[0]
     expert_count = lax.axis_size("dp") * local_experts
     capacity = min(token_count, 2 * token_count * top_count // expert_count)
-    weights = routing_weights / jnp.sum(routing_weights, axis=1, keepdims=True)
     flat_routes = routes.reshape(-1)
     expert_ids = jnp.arange(expert_count, dtype=jnp.int32)
     matches = (flat_routes[:, None] == expert_ids[None, :]).astype(jnp.int32)
@@ -136,6 +468,38 @@
     expert_mix = jnp.sum(weights[:, :, None] * picked, axis=1)
     own_out = (hidden.astype(jnp.float32) + expert_mix).astype(jnp.bfloat16)
     full_out = lax.all_gather(own_out, "tp", axis=1, tiled=True)
+    return own_out, full_out
+
+
+def on_device(
+    hidden,
+    routes,
+    routing_weights,
+    w_gate,
+    w_up,
+    w_down,
+    norm_gain,
+    key_projection_weight,
+    value_projection_weight,
+    queries,
+    cached_key_rows,
+    cached_value_rows,
+    lengths,
+    parents,
+):
+    token_count = hidden.shape[0]
+    expert_count = lax.axis_size("dp") * w_gate.shape[0]
+    weights = routing_weights / jnp.sum(routing_weights, axis=1, keepdims=True)
+    if dense_fits(hidden, routes, w_gate):
+        expert_ids = jnp.arange(expert_count, dtype=jnp.int32)
+        named = routes.T[None, :, :] == expert_ids[:, None, None]
+        shares = jnp.sum(jnp.where(named, weights.T[None, :, :], 0.0), axis=1)
+        shares = jnp.pad(shares, ((0, 0), (0, LANES - token_count)))
+        own_out, full_out = dense_experts(hidden, shares, w_gate, w_up, w_down)
+    else:
+        own_out, full_out = routed_experts(
+            hidden, routes, weights, w_gate, w_up, w_down
+        )
     widened = full_out.astype(jnp.float32)
     scaling = lax.rsqrt(jnp.mean(widened * widened, axis=1, keepdims=True) + 1e-06)
     normed = (widened * scaling * norm_gain).astype(jnp.bfloat16)

time: 291 us -> 100 us (0.34); the launches traced: 286 us -> 100 us
  blocking collectives: 112 us -> 0 us
  waiting for transfers between devices: 93.3 us -> 0 us
  Pallas kernels: 0 us -> 85.8 us
  matrix products: 30.4 us -> 6.18 us
  local copies, waits for them, and re-layouts: 16.4 us -> 2.45 us
  between operations: 15 us -> 1.53 us
  other arithmetic: 12.5 us -> 4.16 us
  starting transfers between devices: 5.74 us -> 0 us
    all_to_all x1 -> x0, blocking collectives: 98 us -> none  [on_device(): lax.all_to_all(outgoing, 'dp', split_axis=0, concat_axis=0, tiled=True)]
    pallas_call x0 -> x1, Pallas kernels: none -> 85.8 us  [dense_experts(): pl.pallas_call(functools.partial(expert_kernel, planes), out_shape=(jax.S...]
    reduce_scatter x1 -> x0, waiting for transfers between devices: 55.2 us -> none  [on_device(): lax.psum_scatter(partial_value.astype(jnp.bfloat16), 'tp', scatter_dimens...]
    all_to_all x1 -> x0, waiting for transfers between devices: 38.1 us -> none  [on_device(): lax.all_to_all(summed.astype(jnp.bfloat16), 'dp', split_axis=0, concat_ax...]
    dot_general x2 -> x0, matrix products: 23.8 us -> none  [the longest x1 17 us: on_device(): jnp.einsum('secf,efd->secd', active, w_down, preferred_element_type=jnp.f...]
    all_gather x2 -> x0, blocking collectives: 14.5 us -> none  [the longest x1 7.42 us: full_rows(): return lax.all_gather(hidden, 'tp', axis=1, tiled=True)]
    gather x2 -> x0, local copies, waits for them, and re-layouts: 10.2 us -> none  [the longest x1 5.83 us: on_device(): jnp.take(flat_back, targets, axis=0)]
    all_to_all x1 -> x0, starting transfers between devices: 5.7 us -> none  [on_device(): lax.all_to_all(summed.astype(jnp.bfloat16), 'dp', split_axis=0, concat_ax...]
  transfers between devices with their start and end apart: 2 -> 0, of which waited for: 2 -> 0; matrix products, arithmetic and copies ran while one was open for 1% -> 0% of each run, Pallas kernels for 0% -> 0%
where the time goes in v1:
time: 100 us
  Pallas kernels  85.8 us (86%)
  matrix products  6.18 us (6%)
  other arithmetic  4.16 us (4%)
  local copies, waits for them, and re-layouts  2.45 us (2%)
  between operations  1.53 us (2%)
    pallas_call x1, Pallas kernels, dense_experts(): pl.pallas_call(functools.partial(expert_kernel, planes), out_shape=(jax.S...  85.8 us

profile of v1, /device:TPU:0, one launch (start us, length us, event | category | flops | bytes accessed | tf_op | source)
XLA Modules:
  0.0 100.1 jit_solution(17129175160992571284)
XLA Ops:
  0.6 0.0 copy-start
  0.6 0.9 reduce_sum.45
  1.5 0.7 divide_bitcast_fusion
  2.2 0.7 select_reduce_fusion
  2.9 0.6 pad.4.share_ref
  3.5 85.8 %dense_experts.1 = (bf16[32,2048]{1,0:T(8,128)(2,1)}, bf16[32,4096]{1,0:T(8,128)(2,1)}) custom-call(bf16[32,2048]{1,0:T(8,128)(2,1)} %hidden_ref.1, f32[16,128]{1,0:T(8,128)} %pad.4.share_ref, bf16[2,8,256,768]{3,2,1,0:T(8,128)(2,1)} %bitcast.53, bf16[2,8,256,768]{3,2,1,0:T(8,128)(2,1)} %bitcast.54, bf16[768,4096]{1,0:T(8,128)(2,1)} %bitcast.55), custom_call_target="tpu_custom_call" | custom-call | tf_op jit(solution)/shard_map/dense_experts/pallas_call | solution.py:315
  89.3 0.0 copy-start.2
  89.3 1.3 %fusion.8 = f32[32]{0:T(128)S(1)} fusion(bf16[32,4096]{1,0:T(8,128)(2,1)} %get-tuple-element.7), kind=kLoop, calls=%fused_computation.21 | loop fusion | flops 393184 | bytes 262272 | tf_op jit(solution)/shard_map/reduce_sum | solution.py:504
  90.6 0.0 copy-done
  90.6 0.0 copy-start.3
  90.6 0.0 copy-start.8
  90.6 1.5 %convolution_convert_fusion.1 = bf16[32,256]{1,0:T(8,128)(2,1)S(1)} fusion(bf16[4096,256]{1,0:T(8,128)(2,1)S(1)} %copy-done, bf16[32,4096]{1,0:T(8,128)(2,1)} %get-tuple-element.7, f32[4096]{0:T(1024)S(1)} %copy-done.5, f32[32]{0:T(128)S(1)} %add_rsqrt_fusion), kind=kOutput, calls=%fused_computation.12 | convolution fusion | flops 67641344 | bytes 2392192 | tf_op jit(solution)/shard_map/dot_general | solution.py:506
  92.1 0.0 copy-done.1
  92.2 0.0 copy-start.6
  92.2 0.0 copy-start.10
  92.2 0.5 convolution_convert_fusion
  92.7 0.0 copy-start.7
  92.7 0.0 copy-start.9
  93.5 0.4 fusion.30
  93.9 0.1 fusion.23
  94.0 0.1 convolution_minimum_fusion.4
  94.1 0.2 convolution_minimum_fusion.2
  94.4 0.2 fusion.7
  94.6 0.1 copy.37
  94.7 0.6 fusion.31
  95.3 0.4 fusion.11
  95.7 0.1 fusion.12
  95.9 1.3 %convolution_bitcast_fusion = f32[2,128,16,32]{1,3,2,0:T(8,128)} fusion(f32[1,2,16,32,128]{4,3,2,1,0:T(8,128)S(1)} %get-tuple-element.9, f32[2,16,32]{2,1,0:T(8,128)S(1)} %add.56, f32[2,16,32]{2,1,0:T(8,128)S(1)} %max.9, bf16[128,2,128,1]{2,1,0,3:T(2,128)(2,1)S(1)} %bitcast.62), kind=kOutput, calls=%fused_computation.1 | convolution fusion | flops 33947648 | bytes 1122304 | tf_op jit(solution)/shard_map/rkgnp,rpkd->rnkgd/dot_general | solution.py:400
  97.1 1.4 %fusion.6 = bf16[1,32,2,16,128]{4,1,3,2,0:T(8,128)(2,1)S(1)} fusion(f32[2,128,16,32]{1,3,2,0:T(8,128)} %convolution_bitcast_fusion, f32[1,2,16,32,32]{3,4,2,1,0:T(8,128)S(1)} %get-tuple-element.11, f32[2,16,32]{2,1,0:T(8,128)S(1)} %add.56, f32[2,16,32]{2,1,0:T(8,128)S(1)} %max.9, bf16[32,2,128,1]{2,1,0,3:T(2,128)(2,1)S(1)} %bitcast.63), kind=kOutput, calls=%fused_computation.10 | convolution fusion | flops 8749056 | bytes 942080 | tf_op jit(solution)/shard_map/rkgnm,rmkd->rnkgd/dot_general | solution.py:403
  98.5 0.1 copy.43
  98.6 0.8 convert_element_type.90
  99.4 0.7 copy.80
  (21 shorter events, 0.2 us)
Async XLA Ops:
  0.6 90.0 %copy-start = (bf16[4096,256]{1,0:T(8,128)(2,1)S(1)}, bf16[4096,256]{1,0:T(8,128)(2,1)}, u32[]{:S(2)}) copy-start(bf16[4096,256]{1,0:T(8,128)(2,1)} %param.21) | copy-start | bytes 6291460
  3.5 87.1 %copy-start.5 = (f32[4096]{0:T(1024)S(1)}, f32[4096]{0:T(1024)}, u32[]{:S(2)}) copy-start(f32[4096]{0:T(1024)} %param.20) | copy-start | bytes 49156
  89.3 2.8 %copy-start.1 = (bf16[32,4096]{1,0:T(8,128)(2,1)S(1)}, bf16[32,4096]{1,0:T(8,128)(2,1)}, u32[]{:S(2)}) copy-start(bf16[32,4096]{1,0:T(8,128)(2,1)} %get-tuple-element.7) | copy-start | bytes 786436
  89.3 2.8 %copy-start.2 = (bf16[4096,256]{1,0:T(8,128)(2,1)S(1)}, bf16[4096,256]{1,0:T(8,128)(2,1)}, u32[]{:S(2)}) copy-start(bf16[4096,256]{1,0:T(8,128)(2,1)} %param.22) | copy-start | bytes 6291460
  90.6 2.1 %copy-start.3 = (bf16[32,4096]{1,0:T(8,128)(2,1)S(1)}, bf16[32,4096]{1,0:T(8,128)(2,1)}, u32[]{:S(2)}) copy-start(bf16[32,4096]{1,0:T(8,128)(2,1)} %param.23) | copy-start | bytes 786436
  90.6 2.1 %copy-start.8 = (bf16[1,128,256]{2,1,0:T(8,128)(2,1)S(1)}, bf16[1,128,256]{2,1,0:T(8,128)(2,1)}, u32[]{:S(2)}) copy-start(bf16[1,128,256]{2,1,0:T(8,128)(2,1)} %param.24) | copy-start | bytes 196612
  92.2 3.1 %copy-start.6 = (bf16[32,256]{1,0:T(8,128)(2,1)}, bf16[32,256]{1,0:T(8,128)(2,1)S(1)}, u32[]{:S(2)}) copy-start(bf16[32,256]{1,0:T(8,128)(2,1)S(1)} %convolution_convert_fusion.1) | copy-start | bytes 49156
  92.2 1.7 %copy-start.10 = (s32[1,32]{1,0:T(1,128)S(1)}, s32[1,32]{1,0:T(1,128)}, u32[]{:S(2)}) copy-start(s32[1,32]{1,0:T(1,128)} %param.27) | copy-start | bytes 388
  92.7 4.4 %copy-start.7 = (bf16[32,256]{1,0:T(8,128)(2,1)}, bf16[32,256]{1,0:T(8,128)(2,1)S(1)}, u32[]{:S(2)}) copy-start(bf16[32,256]{1,0:T(8,128)(2,1)S(1)} %convolution_convert_fusion) | copy-start | bytes 49156
  92.7 3.1 %copy-start.9 = (bf16[1,128,256]{2,1,0:T(8,128)(2,1)S(1)}, bf16[1,128,256]{2,1,0:T(8,128)(2,1)}, u32[]{:S(2)}) copy-start(bf16[1,128,256]{2,1,0:T(8,128)(2,1)} %param.25) | copy-start | bytes 196612
  97.1 2.3 %copy-start.4 = (bf16[32,2048]{1,0:T(8,128)(2,1)S(1)}, bf16[32,2048]{1,0:T(8,128)(2,1)}, u32[]{:S(2)}) copy-start(bf16[32,2048]{1,0:T(8,128)(2,1)} %get-tuple-element.16) | copy-start | bytes 393220

commit v2 on v1

--- a/solution.py
+++ b/solution.py
@@ -158,7 +158,7 @@
 
         lax.fori_loop(0, ff // tile, one, 0)
 
-    for step in range(pieces + 3):
+    for step in range(pieces + 5):
         p = step
         if p < pieces:
             for copy in by_plane[p]:
@@ -170,7 +170,7 @@
                     copy.wait_recv()
                 share_block = shares.at[core, column]
                 share_first = remote(share_block, share_block, over_column)
-        p = step - 1
+        p = step - 2
         if 0 <= p < pieces:
             first[p].wait_recv()
             if p % 2 == 0:
@@ -182,12 +182,12 @@
             if p == 0:
                 share_first.wait_recv()
                 share_across = remote(shares.at[core], shares.at[core], over_core)
-        p = step - 2
+        p = step - 4
         if 0 <= p < pieces:
             second[p].wait_recv()
             block = rows.at[p, :, core]
             across[p] = remote(block, block, over_core)
-        p = step - 3
+        p = step - 5
         if 0 <= p < pieces:
             across[p].wait_recv()
             if p == 0:
@@ -239,7 +239,7 @@
             target[...].astype(jnp.float32) + other[...].astype(jnp.float32)
         ).astype(target.dtype)
 
-    for step in range(pieces + 5):
+    for step in range(pieces + 7):
         p = step
         if p < pieces:
             project(p)
@@ -252,7 +252,7 @@
                 first_moves[p] = remote(mixed.at[p, 1 - side, core], landing, over_side)
             else:
                 first_moves[p] = remote(mixed.at[p, :, core, 1 - column], landing, over_column)
-        p = step - 2
+        p = step - 3
         if 0 <= p < pieces:
             first_moves[p].wait_recv()
             landing = from_second.at[p]
@@ -266,7 +266,7 @@
                 second_moves[p] = remote(
                     mixed.at[p, 1 - side, core, column], landing, over_side
                 )
-        p = step - 3
+        p = step - 5
         if 0 <= p < pieces:
             second_moves[p].wait_recv()
             add(mixed.at[p, side, core, column], from_second.at[p])
@@ -274,7 +274,7 @@
                 remote(mixed.at[p, side, core, column, o], from_plane.at[p, k], where)
                 for k, (o, where) in enumerate(zip(others, over_planes))
             ]
-        p = step - 4
+        p = step - 7
         if 0 <= p < pieces:
             total = mixed[p, side, core, column, plane].astype(jnp.float32)
             for k, copy in enumerate(plane_moves[p]):

time: 100 us -> 86.4 us (0.86)
  Pallas kernels: 85.8 us -> 71.7 us
    pallas_call x1, Pallas kernels: 85.8 us -> 71.7 us  [dense_experts(): pl.pallas_call(functools.partial(expert_kernel, planes), out_shape=(jax.S...]
where the time goes in v2:
time: 86.4 us; the launch traced here: 86 us
  Pallas kernels  71.7 us (83%)
  matrix products  6.18 us (7%)
  other arithmetic  4.16 us (5%)
  local copies, waits for them, and re-layouts  2.45 us (3%)
  between operations  1.53 us (2%)
    pallas_call x1, Pallas kernels, dense_experts(): pl.pallas_call(functools.partial(expert_kernel, planes), out_shape=(jax.S...  71.7 us

profile of v2, /device:TPU:0, one launch (start us, length us, event | category | flops | bytes accessed | tf_op | source)
XLA Modules:
  0.0 86.0 jit_solution(11579393328851439389)
XLA Ops:
  0.6 0.0 copy-start
  0.6 0.9 reduce_sum.45
  1.5 0.7 divide_bitcast_fusion
  2.2 0.7 select_reduce_fusion
  2.9 0.6 pad.4.share_ref
  3.5 71.7 %dense_experts.1 = (bf16[32,2048]{1,0:T(8,128)(2,1)}, bf16[32,4096]{1,0:T(8,128)(2,1)}) custom-call(bf16[32,2048]{1,0:T(8,128)(2,1)} %hidden_ref.1, f32[16,128]{1,0:T(8,128)} %pad.4.share_ref, bf16[2,8,256,768]{3,2,1,0:T(8,128)(2,1)} %bitcast.53, bf16[2,8,256,768]{3,2,1,0:T(8,128)(2,1)} %bitcast.54, bf16[768,4096]{1,0:T(8,128)(2,1)} %bitcast.55), custom_call_target="tpu_custom_call" | custom-call | tf_op jit(solution)/shard_map/dense_experts/pallas_call | solution.py:315
  75.2 0.0 copy-start.2
  75.2 1.3 %fusion.8 = f32[32]{0:T(128)S(1)} fusion(bf16[32,4096]{1,0:T(8,128)(2,1)} %get-tuple-element.7), kind=kLoop, calls=%fused_computation.21 | loop fusion | flops 393184 | bytes 262272 | tf_op jit(solution)/shard_map/reduce_sum | solution.py:504
  76.5 0.0 copy-start.3
  76.5 0.0 copy-start.8
  76.6 1.5 %convolution_convert_fusion.1 = bf16[32,256]{1,0:T(8,128)(2,1)S(1)} fusion(bf16[4096,256]{1,0:T(8,128)(2,1)S(1)} %copy-done, bf16[32,4096]{1,0:T(8,128)(2,1)} %get-tuple-element.7, f32[4096]{0:T(1024)S(1)} %copy-done.5, f32[32]{0:T(128)S(1)} %add_rsqrt_fusion), kind=kOutput, calls=%fused_computation.12 | convolution fusion | flops 67641344 | bytes 2392192 | tf_op jit(solution)/shard_map/dot_general | solution.py:506
  78.0 0.0 copy-done.1
  78.1 0.0 copy-start.6
  78.1 0.0 copy-start.10
  78.1 0.5 convolution_convert_fusion
  78.6 0.0 copy-start.7
  78.6 0.0 copy-start.9
  78.7 0.0 copy-done.8
  79.4 0.4 fusion.30
  79.8 0.1 fusion.23
  79.9 0.1 convolution_minimum_fusion.4
  80.0 0.2 convolution_minimum_fusion.2
  80.3 0.2 fusion.7
  80.5 0.1 copy.37
  80.6 0.6 fusion.31
  81.2 0.4 fusion.11
  81.6 0.1 fusion.12
  81.8 1.3 %convolution_bitcast_fusion = f32[2,128,16,32]{1,3,2,0:T(8,128)} fusion(f32[1,2,16,32,128]{4,3,2,1,0:T(8,128)S(1)} %get-tuple-element.9, f32[2,16,32]{2,1,0:T(8,128)S(1)} %add.56, f32[2,16,32]{2,1,0:T(8,128)S(1)} %max.9, bf16[128,2,128,1]{2,1,0,3:T(2,128)(2,1)S(1)} %bitcast.62), kind=kOutput, calls=%fused_computation.1 | convolution fusion | flops 33947648 | bytes 1122304 | tf_op jit(solution)/shard_map/rkgnp,rpkd->rnkgd/dot_general | solution.py:400
  83.0 1.4 %fusion.6 = bf16[1,32,2,16,128]{4,1,3,2,0:T(8,128)(2,1)S(1)} fusion(f32[2,128,16,32]{1,3,2,0:T(8,128)} %convolution_bitcast_fusion, f32[1,2,16,32,32]{3,4,2,1,0:T(8,128)S(1)} %get-tuple-element.11, f32[2,16,32]{2,1,0:T(8,128)S(1)} %add.56, f32[2,16,32]{2,1,0:T(8,128)S(1)} %max.9, bf16[32,2,128,1]{2,1,0,3:T(2,128)(2,1)S(1)} %bitcast.63), kind=kOutput, calls=%fused_computation.10 | convolution fusion | flops 8749056 | bytes 942080 | tf_op jit(solution)/shard_map/rkgnm,rmkd->rnkgd/dot_general | solution.py:403
  84.4 0.1 copy.43
  84.5 0.8 convert_element_type.90
  85.4 0.7 copy.80
  (21 shorter events, 0.2 us)
Async XLA Ops:
  0.6 75.9 %copy-start = (bf16[4096,256]{1,0:T(8,128)(2,1)S(1)}, bf16[4096,256]{1,0:T(8,128)(2,1)}, u32[]{:S(2)}) copy-start(bf16[4096,256]{1,0:T(8,128)(2,1)} %param.21) | copy-start | bytes 6291460
  3.5 73.0 %copy-start.5 = (f32[4096]{0:T(1024)S(1)}, f32[4096]{0:T(1024)}, u32[]{:S(2)}) copy-start(f32[4096]{0:T(1024)} %param.20) | copy-start | bytes 49156
  75.2 2.8 %copy-start.1 = (bf16[32,4096]{1,0:T(8,128)(2,1)S(1)}, bf16[32,4096]{1,0:T(8,128)(2,1)}, u32[]{:S(2)}) copy-start(bf16[32,4096]{1,0:T(8,128)(2,1)} %get-tuple-element.7) | copy-start | bytes 786436
  75.2 2.8 %copy-start.2 = (bf16[4096,256]{1,0:T(8,128)(2,1)S(1)}, bf16[4096,256]{1,0:T(8,128)(2,1)}, u32[]{:S(2)}) copy-start(bf16[4096,256]{1,0:T(8,128)(2,1)} %param.22) | copy-start | bytes 6291460
  76.5 2.1 %copy-start.3 = (bf16[32,4096]{1,0:T(8,128)(2,1)S(1)}, bf16[32,4096]{1,0:T(8,128)(2,1)}, u32[]{:S(2)}) copy-start(bf16[32,4096]{1,0:T(8,128)(2,1)} %param.23) | copy-start | bytes 786436
  76.5 2.1 %copy-start.8 = (bf16[1,128,256]{2,1,0:T(8,128)(2,1)S(1)}, bf16[1,128,256]{2,1,0:T(8,128)(2,1)}, u32[]{:S(2)}) copy-start(bf16[1,128,256]{2,1,0:T(8,128)(2,1)} %param.24) | copy-start | bytes 196612
  78.1 3.1 %copy-start.6 = (bf16[32,256]{1,0:T(8,128)(2,1)}, bf16[32,256]{1,0:T(8,128)(2,1)S(1)}, u32[]{:S(2)}) copy-start(bf16[32,256]{1,0:T(8,128)(2,1)S(1)} %convolution_convert_fusion.1) | copy-start | bytes 49156
  78.1 1.7 %copy-start.10 = (s32[1,32]{1,0:T(1,128)S(1)}, s32[1,32]{1,0:T(1,128)}, u32[]{:S(2)}) copy-start(s32[1,32]{1,0:T(1,128)} %param.27) | copy-start | bytes 388
  78.6 4.4 %copy-start.7 = (bf16[32,256]{1,0:T(8,128)(2,1)}, bf16[32,256]{1,0:T(8,128)(2,1)S(1)}, u32[]{:S(2)}) copy-start(bf16[32,256]{1,0:T(8,128)(2,1)S(1)} %convolution_convert_fusion) | copy-start | bytes 49156
  78.6 3.1 %copy-start.9 = (bf16[1,128,256]{2,1,0:T(8,128)(2,1)S(1)}, bf16[1,128,256]{2,1,0:T(8,128)(2,1)}, u32[]{:S(2)}) copy-start(bf16[1,128,256]{2,1,0:T(8,128)(2,1)} %param.25) | copy-start | bytes 196612
  83.0 2.3 %copy-start.4 = (bf16[32,2048]{1,0:T(8,128)(2,1)S(1)}, bf16[32,2048]{1,0:T(8,128)(2,1)}, u32[]{:S(2)}) copy-start(bf16[32,2048]{1,0:T(8,128)(2,1)} %get-tuple-element.16) | copy-start | bytes 393220
